TPU v7x, 32 devices: a whole 2x2x4 slice. The times are simulated.
32 devices in a mesh: dp: 4 (over x, y), tp: 8 (over z, core).
Axes of the slice: x: 2, y: 2, z: 4, core: 2. Of those that a mesh axis runs over, the one named last changes fastest.
Arguments:
- x: bfloat16 [15360, 2304], P(('dp', 'tp')), parts along dimension 0
- dy: bfloat16 [15360, 2304], P(('dp', 'tp')), parts along dimension 0
- gate: bfloat16 [15360, 9216], P('dp', 'tp'), parts along dimension 0
- up: bfloat16 [15360, 9216], P('dp', 'tp'), parts along dimension 0
- w_gate: bfloat16 [2304, 9216], P(None, 'tp')
- w_up: bfloat16 [2304, 9216], P(None, 'tp')
- w_down: bfloat16 [9216, 2304], P('tp')
Outputs:
- output 1: bfloat16 [15360, 2304], P(('dp', 'tp')), parts along dimension 0
- output 2: bfloat16 [9216, 9216], P('dp', 'tp'), parts along dimension 0
- output 3: bfloat16 [9216, 9216], P('dp', 'tp'), parts along dimension 0
- output 4: bfloat16 [36864, 2304], P(('dp', 'tp')), parts along dimension 0
There are 4 independent parts. A program takes and returns all parts, laid end to end along the dimension named above; an argument that names none is the same for every part.
All inputs are finite; a program needn't handle non-finite values.
Results may differ from a plain program's by a relative error of at most 0.012.
Values are sent between devices in bfloat16 or wider.
A program may use at most 2 GiB of HBM per device.

v0:
```python
import jax
import jax.numpy as jnp


def act(gate, up):
    return jax.nn.gelu(gate) * up


def solution(mesh):
    def step(x, dy, gate, up, w_gate, w_up, w_down):
        hidden, back = jax.vjp(act, gate.astype(jnp.float32), up.astype(jnp.float32))
        d_hidden = jnp.dot(dy, w_down.T, preferred_element_type=jnp.float32)
        d_gate, d_up = (g.astype(jnp.bfloat16) for g in back(d_hidden))
        dx = jnp.dot(d_gate, w_gate.T) + jnp.dot(d_up, w_up.T)
        groups = mesh.shape["dp"]

        def by_group(a, b):
            a, b = (t.reshape(groups, -1, t.shape[-1]) for t in (a, b))
            product = jnp.einsum("gta,gtb->gab", a, b, preferred_element_type=jnp.float32)
            return product.astype(jnp.bfloat16).reshape(-1, b.shape[-1])

        return dx, by_group(x, d_gate), by_group(x, d_up), by_group(hidden.astype(jnp.bfloat16), dy)

    return step
```

profile of v0, /device:TPU:0, one launch (start us, length us, event | category | flops | bytes accessed | tf_op | source)
XLA Modules:
  0.0 515.1 jit_solution(4111194872917776390)
XLA Ops:
  7.2 0.0 all-gather.11.cloned.1.call-start
  7.2 0.7 all-gather.11.cloned.1.call-update
  7.9 0.0 all-gather.13.cloned.1.call-start
  7.9 0.7 all-gather.13.cloned.1.call-update
  8.6 0.0 reduce-scatter.4.cloned.1.call-start
  8.7 162.3 %all-gather.11.cloned.1.call-done = bf16[3840,2304]{1,0:T(8,128)(2,1)} async-done(((bf16[480,2304]{1,0:T(8,128)(2,1)}), bf16[3840,2304]{1,0:T(8,128)(2,1)}) %all-gather.11.cloned.1.call-update) | async-done | bytes 17694736 | tf_op args[1]
  171.0 43.3 %fusion.4 = (bf16[3840,1152]{1,0:T(8,128)(2,1)}, f32[3840,1152]{1,0:T(8,128)}) fusion(bf16[3840,1152]{1,0:T(8,128)(2,1)} %param.3, bf16[3840,1152]{1,0:T(8,128)(2,1)} %param.2, bf16[3840,2304]{1,0:T(8,128)(2,1)} %all-gather.11.cloned.1.call-done, bf16[1152,2304]{1,0:T(8,128)(2,1)} %param.1), kind=kOutput, calls=%fused_computation.12 | convolution fusion | flops 20486062080 | bytes 67239936 | tf_op jit(solution)/dot_general | solution.py:12
  214.3 29.7 %fusion.21 = bf16[3840,2304]{1,0:T(8,128)(2,1)} fusion(bf16[3840,1152]{1,0:T(8,128)(2,1)} %get-tuple-element.4, bf16[2304,1152]{1,0:T(8,128)(2,1)} %param.4), kind=kOutput, calls=%fused_computation.32 | convolution fusion | flops 20384317440 | bytes 31850496 | tf_op jit(solution)/dot_general | solution.py:14
  244.0 36.1 %convolution_add_fusion = bf16[3840,2304]{1,0:T(8,128)(2,1)} fusion(bf16[3840,2304]{1,0:T(8,128)(2,1)} %fusion.21, bf16[2304,1152]{1,0:T(8,128)(2,1)} %param.5, f32[3840,1152]{1,0:T(8,128)} %get-tuple-element.5, bf16[3840,1152]{1,0:T(8,128)(2,1)} %param.3), kind=kOutput, calls=%fused_computation.8 | convolution fusion | flops 20441825280 | bytes 67239936 | tf_op jit(solution)/dot_general | solution.py:14
  280.1 0.0 reduce-scatter.4.cloned.1.call-update
  280.1 49.9 %all-gather.13.cloned.1.call-done = bf16[3840,2304]{1,0:T(8,128)(2,1)} async-done(((bf16[480,2304]{1,0:T(8,128)(2,1)}), bf16[3840,2304]{1,0:T(8,128)(2,1)}) %all-gather.13.cloned.1.call-update) | async-done | bytes 17694736 | tf_op jit(solution)/reshape | solution.py:18
  330.0 33.7 %fusion.11 = bf16[2304,1152]{0,1:T(8,128)(2,1)} fusion(bf16[3840,2304]{1,0:T(8,128)(2,1)} %all-gather.13.cloned.1.call-done, f32[3840,1152]{1,0:T(8,128)} %get-tuple-element.5, bf16[3840,1152]{1,0:T(8,128)(2,1)} %param.3), kind=kOutput, calls=%fused_computation.23 | convolution fusion | flops 20435632128 | bytes 49545216 | tf_op jit(solution)/gta,gtb->gab/dot_general | solution.py:19
  363.6 8.5 %copy.1 = bf16[2304,1152]{1,0:T(8,128)(2,1)} copy(bf16[2304,1152]{0,1:T(8,128)(2,1)} %fusion.11) | data formatting | bytes 10616832
  372.2 28.3 %fusion.10 = bf16[2304,1152]{0,1:T(8,128)(2,1)} fusion(bf16[3840,1152]{1,0:T(8,128)(2,1)} %get-tuple-element.4, bf16[3840,2304]{1,0:T(8,128)(2,1)} %all-gather.13.cloned.1.call-done), kind=kOutput, calls=%fused_computation.22 | convolution fusion | flops 20386971648 | bytes 31850496 | tf_op jit(solution)/gta,gtb->gab/dot_general | solution.py:19
  400.4 8.5 %copy = bf16[2304,1152]{1,0:T(8,128)(2,1)} copy(bf16[2304,1152]{0,1:T(8,128)(2,1)} %fusion.10) | data formatting | bytes 10616832
  409.0 33.1 %convolution_convert_fusion = bf16[1152,2304]{1,0:T(8,128)(2,1)} fusion(bf16[3840,2304]{1,0:T(8,128)(2,1)} %all-gather.11.cloned.1.call-done, bf16[3840,1152]{1,0:T(8,128)(2,1)} %param.2, bf16[3840,1152]{1,0:T(8,128)(2,1)} %param.3), kind=kOutput, calls=%fused_computation.19 | convolution fusion | flops 20440055808 | bytes 40697856 | tf_op jit(solution)/gta,gtb->gab/dot_general | solution.py:19
  442.1 66.3 %reduce-scatter.4.cloned.1.call-done = bf16[480,2304]{1,0:T(8,128)(2,1)} async-done(((bf16[3840,2304]{1,0:T(8,128)(2,1)}), bf16[480,2304]{1,0:T(8,128)(2,1)}) %reduce-scatter.4.cloned.1.call-update) | async-done | bytes 2211856
Async XLA Ops:
  7.2 163.8 %all-gather.11.cloned.1.call-start = ((), (), s32[]{:S(2)}) async-start(), calls=%async_computation.1 | async-start | bytes 19906560 | tf_op args[1]
  7.9 322.1 %all-gather.13.cloned.1.call-start = ((), (), s32[]{:S(2)}) async-start(), calls=%async_computation.2 | async-start | bytes 19906560 | tf_op jit(solution)/reshape | solution.py:18
  8.6 499.7 %reduce-scatter.4.cloned.1.call-start = ((), (), s32[]{:S(2)}) async-start(), calls=%async_computation.3 | async-start | bytes 19906560
Sparse Core Ops, SparseCore 0:
  9.6 161.3 all-gather.10
  172.6 157.3 all-gather.12
  332.9 175.3 reduce-scatter.3
where the time goes:
time: 522 us; the launch traced here: 515 us
  waiting for transfers between devices  280 us (54%)
  matrix products  204 us (39%)
  local copies, waits for them, and re-layouts  17.1 us (3%)
  between operations  14 us (3%)
    unnamed x5, waiting for transfers between devices  230 us
    dot_general x3, matrix products, by_group(): jnp.einsum('gta,gtb->gab', a, b, preferred_element_type=jnp.float32)  95 us
    dot_general x2, matrix products, step(): dx = jnp.dot(d_gate, w_gate.T) + jnp.dot(d_up, w_up.T)  65.8 us
    reshape x1, waiting for transfers between devices, by_group(): a, b = (t.reshape(groups, -1, t.shape[-1]) for t in (a, b))  49.9 us
    dot_general x1, matrix products, step(): d_hidden = jnp.dot(dy, w_down.T, preferred_element_type=jnp.float32)  43.3 us
    unnamed x2, local copies, waits for them, and re-layouts  17.1 us
  transfers between devices with their start and end apart: 3, of which 3 were waited for; matrix products, arithmetic and copies ran while one was open for 43% of the time, Pallas kernels for 0%

commit v1 on v0

v1 whole, which is shorter than its diff:
```python
import functools

import jax
import jax.numpy as jnp
from jax import lax
from jax.experimental import pallas as pl
from jax.experimental.pallas import tpu as pltpu
from jax.sharding import PartitionSpec as P

MESH = pl.DeviceIdType.MESH
F32, BF16 = jnp.float32, jnp.bfloat16
H = 3


def act(gate, up):
    return jax.nn.gelu(gate) * up


def dot(a, b, ca, cb):
    return lax.dot_general(a, b, (((ca,), (cb,)), ((), ())), preferred_element_type=F32)


def tile_of(n, cap):
    return max(t for t in range(128, min(n, cap) + 1, 128) if n % t == 0)


MID_M = {0: 0, 1: 1, -1: 2, 2: 3}


def kernel(x_ref, dy_ref, gate_ref, up_ref, wg_ref, wu_ref, wd_ref,
           dx_ref, dwg_ref, dwu_ref, dwd_ref,
           dyg, xg, dgs, dus, pown, pin, tst, ru, rv, rw, rso,
           xv, gv, uv, pc, tc, rc, sc, oc,
           sF, sE, rF, rE, sP, rP, sT, rT, sU, rU, sV, rV, sW, rW, lsem):
    S, D = x_ref.shape
    F = gate_ref.shape[1]
    C = S // H
    tp = lax.axis_index("tp")
    z, c = tp // 2, tp % 2
    way = jnp.where(z < 2, 1, -1)
    is_end = (z == 0) | (z == 3)
    is_mid = (z == 1) | (z == 2)

    def chip(k):
        return z + way * k

    def dev(k):
        return {"tp": 2 * chip(k) + c}

    partner = {"tp": 2 * z + 1 - c}
    rows = lambda h: pl.ds(h * C, C)
    given, gathered = (dy_ref, x_ref), (dyg, xg)

    def rcopy(src, dst, ssem, rsem, to):
        return pltpu.make_async_remote_copy(
            src_ref=src, dst_ref=dst, send_sem=ssem, recv_sem=rsem, device_id=to, device_id_type=MESH)

    def local(*copies):
        made = [pltpu.make_async_copy(s, d, lsem.at[i]) for i, (s, d) in enumerate(copies)]
        for cp in made:
            cp.start()
        for cp in made:
            cp.wait()

    def piece(a, k, h):
        return gathered[a].at[2 * chip(k) + c, rows(h)]

    def source(a, k, h):
        return given[a].at[rows(h)] if k == 0 else piece(a, k, h)

    def end_to_f(a, h):
        return rcopy(source(a, 0, h), piece(a, 0, h), sF.at[a, 0, h], rE.at[a, h], dev(1))

    def mid_to_f(a, k, h):
        j = 0 if k == 0 else 1
        return rcopy(source(a, k, h), piece(a, k, h), sF.at[a, j, h], rF.at[a, j, h], dev(1))

    def mid_to_e(a, k, h):
        return rcopy(source(a, k, h), piece(a, k, h), sE.at[a, k, h], rF.at[a, k, h], dev(-1))

    def to_partner(a, k, m):
        src = given[a] if k == 0 else gathered[a].at[2 * chip(k) + c]
        return rcopy(src, gathered[a].at[2 * chip(k) + c], sP.at[a, m], rP.at[a, m], partner)

    def wait_f(a, k, h):
        rcopy(piece(a, k, h), piece(a, k, h), sF.at[a, 0, h], rF.at[a, k - 1, h], partner).wait_recv()

    def wait_e(a, h):
        rcopy(piece(a, -1, h), piece(a, -1, h), sF.at[a, 0, h], rE.at[a, h], partner).wait_recv()

    def term(m):
        return rcopy(tst.at[m], pin.at[m], sT.at[m], rT.at[m], partner)

    def u_copy(j, h):
        return rcopy(rso.at[j, rows(h)], ru.at[j, rows(h)], sU.at[j, h], rU.at[j, h], dev(1))

    def v_copy(j, h):
        return rcopy(rso.at[j, rows(h)], rv.at[j, rows(h)], sV.at[j, h], rV.at[j, h], dev(1))

    def w_copy(h):
        return rcopy(rso.at[2, rows(h)], rw.at[rows(h)], sW.at[h], rW.at[h], dev(-1))

    def combine(m, h, received, out):
        bufs = [pc, tc, rc, sc]
        srcs = [pown.at[m, rows(h)], pin.at[m, rows(h)], *received]
        local(*zip(srcs, bufs))
        step = 16

        @pl.loop(0, C // step)
        def _(i):
            r = pl.ds(pl.multiple_of(i * step, step), step)
            total = pc[r, :] + tc[r, :].astype(F32)
            for b in bufs[2:len(srcs)]:
                total += b[r, :].astype(F32)
            oc[r, :] = total.astype(BF16)

        local((oc, out))

    barrier = pltpu.get_barrier_semaphore()
    pl.semaphore_signal(barrier, inc=1, device_id=partner, device_id_type=MESH)
    pl.semaphore_signal(barrier, inc=1, device_id=dev(1), device_id_type=MESH)

    @pl.when(is_mid)
    def _():
        pl.semaphore_signal(barrier, inc=1, device_id=dev(-1), device_id_type=MESH)
        pl.semaphore_wait(barrier, 3)

    @pl.when(is_end)
    def _():
        pl.semaphore_wait(barrier, 2)

    @pl.when(is_mid)
    def _():
        for h in range(H):
            mid_to_e(0, 0, h).start()
            mid_to_f(0, 0, h).start()

    @pl.when(is_end)
    def _():
        for h in range(H):
            end_to_f(0, h).start()
        for h in range(H):
            end_to_f(1, h).start()

    for a in range(2):
        to_partner(a, 0, 0).start()

    def k_of(m):
        mid = jnp.where(m == 2, -1, jnp.where(m == 3, 2, m))
        return jnp.where(is_end, m, mid)

    def load_shard(a, m, p):
        t = 2 * (z + way * k_of(m)) + jnp.where(p == 0, c, 1 - c)

        @pl.when(p == 1)
        def _():
            rcopy(gathered[a].at[t], gathered[a].at[t], sP.at[a, m], rP.at[a, m], partner).wait_recv()

        @pl.when((m == 0) & (p == 0))
        def _():
            pltpu.make_async_copy(given[a], xv, lsem.at[2]).start()

        @pl.when((m > 0) | (p > 0))
        def _():
            pltpu.make_async_copy(gathered[a].at[t], xv, lsem.at[2]).start()

        return t

    def phase1(wd, wg, wu, accd, hid, dgv, duv, dxf, dxb, stage):
        local((wd_ref, wd), (wg_ref, wg))
        local((wu_ref, wu))
        accd[...] = jnp.zeros_like(accd)

        def unit(m, p):
            t = load_shard(0, m, p)
            local((gate_ref.at[pl.ds(t * S, S)], gv), (up_ref.at[pl.ds(t * S, S)], uv))
            pltpu.make_async_copy(given[0], xv, lsem.at[2]).wait()
            tn = min(F, 256)

            @pl.loop(0, pl.cdiv(F, tn))
            def _(n):
                s = pl.ds(pl.multiple_of(jnp.minimum(n * tn, F - tn), 128), tn)
                d_hidden = dot(xv[...], wd[s, :], 1, 1)
                hidden, back = jax.vjp(act, gv[:, s].astype(F32), uv[:, s].astype(F32))
                d_gate, d_up = back(d_hidden)
                hid[:, s] = hidden.astype(BF16)
                dgv[:, s] = d_gate.astype(BF16)
                duv[:, s] = d_up.astype(BF16)

            keep = [pltpu.make_async_copy(v, o.at[2 * m + p], lsem.at[i])
                    for i, (v, o) in enumerate(((dgv, dgs), (duv, dus)))]
            for cp in keep:
                cp.start()
            tn2 = tile_of(D, 256)

            @pl.loop(0, D // tn2)
            def _(n):
                s = pl.ds(pl.multiple_of(n * tn2, tn2), tn2)
                part = dot(dgv[...], wg[s, :], 1, 1) + dot(duv[...], wu[s, :], 1, 1)
                dxf[:, s] = part
                dxb[:, s] = part.astype(BF16)

            for cp in keep:
                cp.wait()

            @pl.when(p == 0)
            def _():
                local((dxf, pown.at[m]))

            @pl.when(p == 1)
            def _():
                local((dxb, tst.at[m]))
                term(m).start()

            tn3 = tile_of(D, 768)

            @pl.loop(0, D // tn3)
            def _(n):
                s = pl.ds(pl.multiple_of(n * tn3, tn3), tn3)
                accd[:, s] += dot(hid[...], xv[:, s], 0, 0)

        def wait_term(m):
            term(m).wait_recv()

        def send_u(j):
            wait_term(j + 1)
            for h in range(H):
                combine(j + 1, h, [], rso.at[j, rows(h)])
                u_copy(j, h).start()

        @pl.loop(0, 4)
        def _(m):
            @pl.loop(0, 2)
            def _(p):
                unit(m, p)

            @pl.when((m == 0) & is_end)
            def _():
                for h in range(H):
                    wait_f(0, 1, h)
                to_partner(0, 1, 1).start()

            @pl.when((m == 0) & is_mid)
            def _():
                for h in range(H):
                    wait_f(0, 1, h)
                    mid_to_e(0, 1, h).start()
                    wait_e(0, h)
                    mid_to_f(0, -1, h).start()
                to_partner(0, 1, 1).start()
                to_partner(0, -1, 2).start()
                for h in range(H):
                    mid_to_f(1, 0, h).start()

            @pl.when((m == 1) & is_end)
            def _():
                send_u(0)
                for h in range(H):
                    wait_f(0, 2, h)
                to_partner(0, 2, 2).start()

            @pl.when((m == 1) & is_mid)
            def _():
                for h in range(H):
                    wait_f(0, 2, h)
                    mid_to_e(0, 2, h).start()
                to_partner(0, 2, 3).start()
                for h in range(H):
                    mid_to_e(1, 0, h).start()
                for h in range(H):
                    wait_e(1, h)
                    mid_to_f(1, -1, h).start()
                to_partner(1, -1, 2).start()

            @pl.when((m == 2) & is_end)
            def _():
                send_u(1)
                for h in range(H):
                    wait_f(0, 3, h)
                to_partner(0, 3, 3).start()

            @pl.when((m == 2) & is_mid)
            def _():
                for h in range(H):
                    wait_f(1, 1, h)
                    mid_to_e(1, 1, h).start()
                to_partner(1, 1, 1).start()

            @pl.when((m == 3) & is_end)
            def _():
                send_u(2)

        flush(accd, dwd_ref, stage)

    def flush(acc, out, stage):
        n = stage.shape[0]

        @pl.loop(0, acc.shape[0] // n)
        def _(i):
            r = pl.ds(pl.multiple_of(i * n, n), n)
            stage[...] = acc[r, :].astype(BF16)
            local((stage, out.at[r]))

    def send_v(j):
        m = MID_M[j + 1]
        term(m).wait_recv()
        for h in range(H):
            rcopy(ru.at[j + 1, rows(h)], ru.at[j + 1, rows(h)], sU.at[j + 1, h], rU.at[j + 1, h], partner).wait_recv()
            combine(m, h, [ru.at[j + 1, rows(h)]], rso.at[j, rows(h)])
            v_copy(j, h).start()

    def send_w():
        m = MID_M[-1]
        term(m).wait_recv()
        for h in range(H):
            rcopy(rv.at[1, rows(h)], rv.at[1, rows(h)], sV.at[1, h], rV.at[1, h], partner).wait_recv()
            combine(m, h, [rv.at[1, rows(h)]], rso.at[2, rows(h)])
            w_copy(h).start()

    def phase2(accg, accu, stage):
        accg[...] = jnp.zeros_like(accg)
        accu[...] = jnp.zeros_like(accu)

        def unit(m, p):
            load_shard(1, m, p)
            local((dgs.at[2 * m + p], gv), (dus.at[2 * m + p], uv))
            pltpu.make_async_copy(given[1], xv, lsem.at[2]).wait()
            tm = tile_of(D, 768)

            @pl.loop(0, D // tm)
            def _(n):
                s = pl.ds(pl.multiple_of(n * tm, tm), tm)
                accg[s, :] += dot(xv[:, s], gv[...], 0, 0)
                accu[s, :] += dot(xv[:, s], uv[...], 0, 0)

        @pl.loop(0, 4)
        def _(m):
            @pl.when((m == 0) & is_mid)
            def _():
                send_v(0)

            @pl.when((m == 1) & is_mid)
            def _():
                for h in range(H):
                    wait_f(1, 2, h)
                    mid_to_e(1, 2, h).start()
                to_partner(1, 2, 3).start()

            @pl.when((m == 3) & is_mid)
            def _():
                send_v(1)

            for i in range(1, 4):
                @pl.when((m == i) & is_end)
                def _(i=i):
                    for h in range(H):
                        wait_f(1, i, h)
                    to_partner(1, i, i).start()

            @pl.loop(0, 2)
            def _(p):
                unit(m, p)

        @pl.when(is_mid)
        def _():
            send_w()

        flush(accg, dwg_ref, stage)
        flush(accu, dwu_ref, stage)

    wbuf = lambda r: pltpu.VMEM(r.shape, r.dtype)
    pl.run_scoped(
        phase1, wbuf(wd_ref), wbuf(wg_ref), wbuf(wu_ref), pltpu.VMEM((F, D), F32),
        pltpu.VMEM((S, F), BF16), pltpu.VMEM((S, F), BF16), pltpu.VMEM((S, F), BF16),
        pltpu.VMEM((S, D), F32), pltpu.VMEM((S, D), BF16), pltpu.VMEM((tile_of(F, 384), D), BF16))
    pl.run_scoped(
        phase2, pltpu.VMEM((D, F), F32), pltpu.VMEM((D, F), F32), pltpu.VMEM((tile_of(D, 768), F), BF16))

    term(0).wait_recv()

    @pl.when(is_mid)
    def _():
        for h in range(H):
            rcopy(ru.at[0, rows(h)], ru.at[0, rows(h)], sU.at[0, h], rU.at[0, h], partner).wait_recv()
            rcopy(rv.at[0, rows(h)], rv.at[0, rows(h)], sV.at[0, h], rV.at[0, h], partner).wait_recv()
            combine(0, h, [ru.at[0, rows(h)], rv.at[0, rows(h)]], dx_ref.at[rows(h)])

    @pl.when(is_end)
    def _():
        for h in range(H):
            rcopy(rw.at[rows(h)], rw.at[rows(h)], sW.at[h], rW.at[h], partner).wait_recv()
            combine(0, h, [rw.at[rows(h)]], dx_ref.at[rows(h)])

    for m in range(4):
        term(m).wait_send()

    @pl.when(is_end)
    def _():
        for a in range(2):
            for h in range(H):
                end_to_f(a, h).wait_send()
            for k in range(4):
                to_partner(a, k, k).wait_send()
        for j in range(3):
            for h in range(H):
                u_copy(j, h).wait_send()

    @pl.when(is_mid)
    def _():
        for a in range(2):
            for h in range(H):
                for k in (0, 1, 2):
                    mid_to_e(a, k, h).wait_send()
                for k in (0, -1):
                    mid_to_f(a, k, h).wait_send()
            for k, m in MID_M.items():
                to_partner(a, k, m).wait_send()
        for h in range(H):
            for j in range(2):
                v_copy(j, h).wait_send()
            w_copy(h).wait_send()


def solution(mesh):
    def step(x, dy, gate, up, w_gate, w_up, w_down):
        (S, D), F = x.shape, gate.shape[1]
        C = S // H
        shape = jax.ShapeDtypeStruct
        any_ = pl.BlockSpec(memory_space=pl.ANY)
        outs = [
            shape((S, D), BF16), shape((D, F), BF16), shape((D, F), BF16), shape((F, D), BF16),
            shape((8, S, D), BF16), shape((8, S, D), BF16),
            shape((8, S, F), BF16), shape((8, S, F), BF16),
            shape((4, S, D), F32), shape((4, S, D), BF16), shape((4, S, D), BF16),
            shape((3, S, D), BF16), shape((2, S, D), BF16), shape((S, D), BF16), shape((3, S, D), BF16),
        ]
        dma = pltpu.SemaphoreType.DMA
        out = pl.pallas_call(
            kernel,
            out_shape=outs,
            in_specs=[any_] * 7,
            out_specs=[any_] * len(outs),
            scratch_shapes=[
                pltpu.VMEM((S, D), BF16), pltpu.VMEM((S, F), BF16), pltpu.VMEM((S, F), BF16),
                pltpu.VMEM((C, D), F32), pltpu.VMEM((C, D), BF16), pltpu.VMEM((C, D), BF16),
                pltpu.VMEM((C, D), BF16), pltpu.VMEM((C, D), BF16),
                dma((2, 2, H)), dma((2, 3, H)), dma((2, 3, H)), dma((2, H)),
                dma((2, 4)), dma((2, 4)), dma((4,)), dma((4,)),
                dma((3, H)), dma((3, H)), dma((2, H)), dma((2, H)), dma((H,)), dma((H,)),
                dma((4,)),
            ],
            compiler_params=pltpu.CompilerParams(
                collective_id=0, has_side_effects=True, vmem_limit_bytes=60 * 2**20),
            name="mlp_backward",
        )(x, dy, gate, up, w_gate, w_up, w_down)
        return tuple(out[:4])

    both = P(("dp", "tp"), None)
    cols = P("dp", "tp")
    return jax.shard_map(
        step, mesh=mesh,
        in_specs=(both, both, cols, cols, P(None, "tp"), P(None, "tp"), P("tp", None)),
        out_specs=(both, cols, cols, both), check_vma=False)
```

time: 522 us -> 358 us (0.69); the launches traced: 515 us -> 357 us
  Pallas kernels: 0 us -> 341 us
  waiting for transfers between devices: 280 us -> 0 us
  matrix products: 204 us -> 0 us
  between operations: 14 us -> 0.65 us
    pallas_call x0 -> x1, Pallas kernels: none -> 341 us  [step(): pl.pallas_call(kernel, out_shape=outs, in_specs=[any_] * 7, out_specs=[an...]
    unnamed x5 -> x0, waiting for transfers between devices: 230 us -> none
    dot_general x6 -> x0, matrix products: 204 us -> none  [the longest x3 95 us: by_group(): jnp.einsum('gta,gtb->gab', a, b, preferred_element_type=jnp.float32)]
    reshape x1 -> x0, waiting for transfers between devices: 49.9 us -> none  [by_group(): a, b = (t.reshape(groups, -1, t.shape[-1]) for t in (a, b))]
    unnamed x2 -> x10, local copies, waits for them, and re-layouts: 17.1 us -> 15.1 us
  transfers between devices with their start and end apart: 3 -> 0, of which waited for: 3 -> 0; matrix products, arithmetic and copies ran while one was open for 43% -> 0% of each run, Pallas kernels for 0% -> 0%
where the time goes in v1:
time: 358 us; the launch traced here: 357 us
  Pallas kernels  341 us (95%)
  local copies, waits for them, and re-layouts  15.1 us (4%)
    pallas_call x1, Pallas kernels, step(): pl.pallas_call(kernel, out_shape=outs, in_specs=[any_] * 7, out_specs=[an...  341 us
    unnamed x10, local copies, waits for them, and re-layouts  15.1 us

profile of v1, /device:TPU:0, one launch (start us, length us, event | category | flops | bytes accessed | tf_op | source)
XLA Modules:
  0.0 357.1 jit_solution(8922276239165250059)
XLA Ops:
  0.6 341.4 %mlp_backward.1 = (bf16[480,2304]{1,0:T(8,128)(2,1)}, bf16[2304,1152]{1,0:T(8,128)(2,1)}, bf16[2304,1152]{1,0:T(8,128)(2,1)}, bf16[1152,2304]{1,0:T(8,128)(2,1)}...) custom-call(bf16[480,2304]{1,0:T(8,128)(2,1)} %x_ref.1, ...), custom_call_target="tpu_custom_call" | custom-call | tf_op jit(solution)/shard_map/mlp_backward/pallas_call | solution.py:438
  342.1 3.1 copy.15
  345.2 0.0 copy-start
  345.2 0.0 slice-start
  345.2 5.8 %copy.16 = bf16[2304,1152]{1,0:T(8,128)(2,1)} copy(bf16[2304,1152]{1,0:T(8,128)(2,1)} %get-tuple-element.17) | data formatting | bytes 10616832
  351.0 0.0 copy-done
  351.0 0.0 slice-start.1
  351.0 2.7 copy.17
  353.7 0.0 slice-done
  353.7 1.1 slice-done.1
  354.8 2.4 copy.18
  (1 shorter events, 0.0 us)
Async XLA Ops:
  345.2 5.8 %copy-start = (bf16[2304,1152]{1,0:T(8,128)(2,1)S(1)}, bf16[2304,1152]{1,0:T(8,128)(2,1)}, u32[]{:S(2)}) copy-start(bf16[2304,1152]{1,0:T(8,128)(2,1)} %get-tuple-element.18) | copy-start | bytes 15925252
  345.2 8.5 %slice-start = ((s8[5308416]{0:T(1024)(128)(4,1)}), s8[4194304]{0:T(1024)(128)(4,1)S(1)}, s32[]{:S(2)}) async-start(s8[5308416]{0:T(1024)(128)(4,1)} %bitcast), calls=%async_computation | async-start | bytes 8388608
  351.0 3.8 %slice-start.1 = ((s8[5308416]{0:T(1024)(128)(4,1)}), s8[1114112]{0:T(1024)(128)(4,1)S(1)}, s32[]{:S(2)}) async-start(s8[5308416]{0:T(1024)(128)(4,1)} %bitcast), calls=%async_computation.1 | async-start | bytes 2228224

commit v2 on v1

--- a/solution.py
+++ b/solution.py
@@ -28,9 +28,9 @@
 
 
 def kernel(x_ref, dy_ref, gate_ref, up_ref, wg_ref, wu_ref, wd_ref,
-           dx_ref, dwg_ref, dwu_ref, dwd_ref,
-           dyg, xg, dgs, dus, pown, pin, tst, ru, rv, rw, rso,
-           xv, gv, uv, pc, tc, rc, sc, oc,
+           base_ref, dwg_ref, dwu_ref, dwd_ref, rw, wlast,
+           dyg, xg, dgs, dus, pown, pin, tst, ru, rv, rso,
+           xv, gv, uv, pc, tc, rc, sc, oc, fc,
            sF, sE, rF, rE, sP, rP, sT, rT, sU, rU, sV, rV, sW, rW, lsem):
     S, D = x_ref.shape
     F = gate_ref.shape[1]
@@ -100,7 +100,7 @@
     def w_copy(h):
         return rcopy(rso.at[2, rows(h)], rw.at[rows(h)], sW.at[h], rW.at[h], dev(-1))
 
-    def combine(m, h, received, out):
+    def combine(m, h, received, out, res=oc):
         bufs = [pc, tc, rc, sc]
         srcs = [pown.at[m, rows(h)], pin.at[m, rows(h)], *received]
         local(*zip(srcs, bufs))
@@ -112,9 +112,9 @@
             total = pc[r, :] + tc[r, :].astype(F32)
             for b in bufs[2:len(srcs)]:
                 total += b[r, :].astype(F32)
-            oc[r, :] = total.astype(BF16)
-
-        local((oc, out))
+            res[r, :] = total.astype(res.dtype)
+
+        local((res, out))
 
     barrier = pltpu.get_barrier_semaphore()
     pl.semaphore_signal(barrier, inc=1, device_id=partner, device_id_type=MESH)
@@ -290,16 +290,35 @@
             def _():
                 send_u(2)
 
-        flush(accd, dwd_ref, stage)
-
-    def flush(acc, out, stage):
-        n = stage.shape[0]
-
-        @pl.loop(0, acc.shape[0] // n)
-        def _(i):
-            r = pl.ds(pl.multiple_of(i * n, n), n)
-            stage[...] = acc[r, :].astype(BF16)
-            local((stage, out.at[r]))
+        flush([(accd, dwd_ref)], stage)
+
+    def flush(pairs, stage):
+        n = stage.shape[1]
+        jobs = [(acc, out, r) for acc, out in pairs for r in range(0, acc.shape[0], n)]
+        made = []
+        for i, (acc, out, r) in enumerate(jobs):
+            if i >= 2:
+                made[i - 2].wait()
+            stage[i % 2] = acc[r:r + n, :].astype(BF16)
+            made.append(pltpu.make_async_copy(stage.at[i % 2], out.at[pl.ds(r, n)], lsem.at[i % 2]))
+            made[i].start()
+        for cp in made[-2:]:
+            cp.wait()
+
+    def own_rows():
+        term(0).wait_recv()
+
+        @pl.when(is_mid)
+        def _():
+            for h in range(H):
+                rcopy(ru.at[0, rows(h)], ru.at[0, rows(h)], sU.at[0, h], rU.at[0, h], partner).wait_recv()
+                rcopy(rv.at[0, rows(h)], rv.at[0, rows(h)], sV.at[0, h], rV.at[0, h], partner).wait_recv()
+                combine(0, h, [ru.at[0, rows(h)], rv.at[0, rows(h)]], base_ref.at[rows(h)], fc)
+
+        @pl.when(is_end)
+        def _():
+            for h in range(H):
+                combine(0, h, [], base_ref.at[rows(h)], fc)
 
     def send_v(j):
         m = MID_M[j + 1]
@@ -314,8 +333,9 @@
         term(m).wait_recv()
         for h in range(H):
             rcopy(rv.at[1, rows(h)], rv.at[1, rows(h)], sV.at[1, h], rV.at[1, h], partner).wait_recv()
-            combine(m, h, [rv.at[1, rows(h)]], rso.at[2, rows(h)])
-            w_copy(h).start()
+            combine(m, h, [rv.at[1, rows(h)]], rso.at[2, rows(h)] if h < H - 1 else wlast)
+            if h < H - 1:
+                w_copy(h).start()
 
     def phase2(accg, accu, stage):
         accg[...] = jnp.zeros_like(accg)
@@ -349,6 +369,10 @@
             @pl.when((m == 3) & is_mid)
             def _():
                 send_v(1)
+
+            @pl.when(m == 3)
+            def _():
+                own_rows()
 
             for i in range(1, 4):
                 @pl.when((m == i) & is_end)
@@ -365,31 +389,20 @@
         def _():
             send_w()
 
-        flush(accg, dwg_ref, stage)
-        flush(accu, dwu_ref, stage)
+        flush([(accg, dwg_ref), (accu, dwu_ref)], stage)
 
     wbuf = lambda r: pltpu.VMEM(r.shape, r.dtype)
     pl.run_scoped(
         phase1, wbuf(wd_ref), wbuf(wg_ref), wbuf(wu_ref), pltpu.VMEM((F, D), F32),
         pltpu.VMEM((S, F), BF16), pltpu.VMEM((S, F), BF16), pltpu.VMEM((S, F), BF16),
-        pltpu.VMEM((S, D), F32), pltpu.VMEM((S, D), BF16), pltpu.VMEM((tile_of(F, 384), D), BF16))
+        pltpu.VMEM((S, D), F32), pltpu.VMEM((S, D), BF16), pltpu.VMEM((2, tile_of(F, 128), D), BF16))
     pl.run_scoped(
-        phase2, pltpu.VMEM((D, F), F32), pltpu.VMEM((D, F), F32), pltpu.VMEM((tile_of(D, 768), F), BF16))
-
-    term(0).wait_recv()
-
-    @pl.when(is_mid)
-    def _():
-        for h in range(H):
-            rcopy(ru.at[0, rows(h)], ru.at[0, rows(h)], sU.at[0, h], rU.at[0, h], partner).wait_recv()
-            rcopy(rv.at[0, rows(h)], rv.at[0, rows(h)], sV.at[0, h], rV.at[0, h], partner).wait_recv()
-            combine(0, h, [ru.at[0, rows(h)], rv.at[0, rows(h)]], dx_ref.at[rows(h)])
+        phase2, pltpu.VMEM((D, F), F32), pltpu.VMEM((D, F), F32), pltpu.VMEM((2, tile_of(D, 256), F), BF16))
 
     @pl.when(is_end)
     def _():
-        for h in range(H):
+        for h in range(H - 1):
             rcopy(rw.at[rows(h)], rw.at[rows(h)], sW.at[h], rW.at[h], partner).wait_recv()
-            combine(0, h, [rw.at[rows(h)]], dx_ref.at[rows(h)])
 
     for m in range(4):
         term(m).wait_send()
@@ -418,7 +431,56 @@
         for h in range(H):
             for j in range(2):
                 v_copy(j, h).wait_send()
+        for h in range(H - 1):
             w_copy(h).wait_send()
+
+
+def finish_kernel(base, part, gate_in, up_in, down_in, dx, gate_out, up_out, down_out, gv, uv, dv, bv, pv, ov, isem, osem):
+    n = part.shape[0]
+    bring = [pltpu.make_async_copy(base.at[pl.ds(0, n)], bv, isem.at[0]), pltpu.make_async_copy(part, pv, isem.at[1])]
+    put = []
+    for src, v, dst in ((gate_in, gv, gate_out), (up_in, uv, up_out), (down_in, dv, down_out)):
+        size = src.shape[0] // 3
+        for r in range(3):
+            piece = pl.ds(r * size, size)
+            bring.append(pltpu.make_async_copy(src.at[piece], v.at[piece], isem.at[len(bring)]))
+            put.append(pltpu.make_async_copy(v.at[piece], dst.at[piece], osem.at[len(put)]))
+    for cp in bring:
+        cp.start()
+    bring[0].wait()
+    bring[1].wait()
+    tp = lax.axis_index("tp")
+    is_end = (tp < 2) | (tp >= 6)
+    step = 16
+
+    @pl.loop(0, n // step)
+    def _(i):
+        r = pl.ds(pl.multiple_of(i * step, step), step)
+        ov[r, :] = (bv[r, :] + jnp.where(is_end, pv[r, :].astype(F32), 0.0)).astype(BF16)
+
+    put.append(pltpu.make_async_copy(ov, dx.at[pl.ds(0, n)], osem.at[len(put)]))
+    put[-1].start()
+    for got, cp in zip(bring[2:], put):
+        got.wait()
+        cp.start()
+    for cp in put:
+        cp.wait()
+
+
+def finish(base, part, *grads):
+    S, D = base.shape
+    any_ = pl.BlockSpec(memory_space=pl.ANY)
+    n = part.shape[0]
+    moved = 2 * sum(g.size * 2 for g in grads)
+    return pl.pallas_call(
+        finish_kernel, in_specs=[any_] * 5, out_specs=[any_] * 4,
+        out_shape=[jax.ShapeDtypeStruct((S, D), BF16)] + [jax.ShapeDtypeStruct(g.shape, BF16) for g in grads],
+        scratch_shapes=[pltpu.VMEM(g.shape, BF16) for g in grads] + [
+            pltpu.VMEM((n, D), F32), pltpu.VMEM((n, D), BF16), pltpu.VMEM((n, D), BF16),
+            pltpu.SemaphoreType.DMA((11,)), pltpu.SemaphoreType.DMA((10,))],
+        compiler_params=pltpu.CompilerParams(vmem_limit_bytes=62 * 2**20),
+        cost_estimate=pl.CostEstimate(flops=10**9, bytes_accessed=moved, transcendentals=0),
+        name="finish")(base, part, *grads)
 
 
 def solution(mesh):
@@ -428,11 +490,12 @@
         shape = jax.ShapeDtypeStruct
         any_ = pl.BlockSpec(memory_space=pl.ANY)
         outs = [
-            shape((S, D), BF16), shape((D, F), BF16), shape((D, F), BF16), shape((F, D), BF16),
+            shape((S, D), F32), shape((D, F), BF16), shape((D, F), BF16), shape((F, D), BF16),
+            shape((S - C, D), BF16), shape((C, D), BF16),
             shape((8, S, D), BF16), shape((8, S, D), BF16),
             shape((8, S, F), BF16), shape((8, S, F), BF16),
             shape((4, S, D), F32), shape((4, S, D), BF16), shape((4, S, D), BF16),
-            shape((3, S, D), BF16), shape((2, S, D), BF16), shape((S, D), BF16), shape((3, S, D), BF16),
+            shape((3, S, D), BF16), shape((2, S, D), BF16), shape((3, S, D), BF16),
         ]
         dma = pltpu.SemaphoreType.DMA
         out = pl.pallas_call(
@@ -443,7 +506,7 @@
             scratch_shapes=[
                 pltpu.VMEM((S, D), BF16), pltpu.VMEM((S, F), BF16), pltpu.VMEM((S, F), BF16),
                 pltpu.VMEM((C, D), F32), pltpu.VMEM((C, D), BF16), pltpu.VMEM((C, D), BF16),
-                pltpu.VMEM((C, D), BF16), pltpu.VMEM((C, D), BF16),
+                pltpu.VMEM((C, D), BF16), pltpu.VMEM((C, D), BF16), pltpu.VMEM((C, D), F32),
                 dma((2, 2, H)), dma((2, 3, H)), dma((2, 3, H)), dma((2, H)),
                 dma((2, 4)), dma((2, 4)), dma((4,)), dma((4,)),
                 dma((3, H)), dma((3, H)), dma((2, H)), dma((2, H)), dma((H,)), dma((H,)),
@@ -453,7 +516,12 @@
                 collective_id=0, has_side_effects=True, vmem_limit_bytes=60 * 2**20),
             name="mlp_backward",
         )(x, dy, gate, up, w_gate, w_up, w_down)
-        return tuple(out[:4])
+        base, dwg, dwu, dwd, early, last = out[:6]
+        last = lax.ppermute(last, "tp", [(2, 0), (3, 1), (4, 6), (5, 7)])
+        dx, *grads = finish(base, early, dwg, dwu, dwd)
+        done = S - C
+        dx = lax.dynamic_update_slice(dx, (base[done:] + last.astype(F32)).astype(BF16), (done, 0))
+        return dx, *grads
 
     both = P(("dp", "tp"), None)
     cols = P("dp", "tp")

time: 358 us -> 353 us (0.986)
  local copies, waits for them, and re-layouts: 15.1 us -> 0 us
  Pallas kernels: 341 us -> 345 us
    unnamed x10 -> x0, local copies, waits for them, and re-layouts: 15.1 us -> none
    pallas_call x0 -> x1, Pallas kernels: none -> 13.1 us  [finish(): pl.pallas_call(finish_kernel, in_specs=[any_] * 5, out_specs=[any_] * 4,...]
    pallas_call x1, Pallas kernels: 341 us -> 332 us  [step(): pl.pallas_call(kernel, out_shape=outs, in_specs=[any_] * 7, out_specs=[an...]
  transfers between devices with their start and end apart: 0 -> 1, of which waited for: 0 -> 1; matrix products, arithmetic and copies ran while one was open for 0% -> 0% of each run, Pallas kernels for 0% -> 4%
where the time goes in v2:
time: 353 us
  Pallas kernels  345 us (98%)
    pallas_call x1, Pallas kernels, step(): pl.pallas_call(kernel, out_shape=outs, in_specs=[any_] * 7, out_specs=[an...  332 us
    pallas_call x1, Pallas kernels, finish(): pl.pallas_call(finish_kernel, in_specs=[any_] * 5, out_specs=[any_] * 4,...  13.1 us
  transfers between devices with their start and end apart: 1, of which 1 were waited for; matrix products, arithmetic and copies ran while one was open for 0% of the time, Pallas kernels for 4%

profile of v2, /device:TPU:0, one launch (start us, length us, event | category | flops | bytes accessed | tf_op | source)
XLA Modules:
  0.0 352.8 jit_solution(12529393706846679826)
XLA Ops:
  0.6 332.1 %mlp_backward.1 = (f32[480,2304]{1,0:T(8,128)}, bf16[2304,1152]{1,0:T(8,128)(2,1)}, bf16[2304,1152]{1,0:T(8,128)(2,1)}, bf16[1152,2304]{1,0:T(8,128)(2,1)}, bf16...) custom-call(bf16[480,2304]{1,0:T(8,128)(2,1)} %x_ref.1, ...), custom_call_target="tpu_custom_call" | custom-call | tf_op jit(solution)/shard_map/mlp_backward/pallas_call | solution.py:501
  332.7 1.3 collective-permute-start
  334.0 13.1 %finish.1 = (bf16[480,2304]{1,0:T(8,128)(2,1)}, bf16[2304,1152]{1,0:T(8,128)(2,1)}, bf16[2304,1152]{1,0:T(8,128)(2,1)}, bf16[1152,2304]{1,0:T(8,128)(2,1)}) custom-call(f32[480,2304]{1,0:T(8,128)} %get-tuple-element.14.base, bf16[320,2304]{1,0:T(8,128)(2,1)} %get-tuple-element.15.part, bf16[2304,1152]{1,0:T(8,128)(2,1)} %get-tuple-element.16.gate_in, ...), custom_call_target="tpu_custom_call" | custom-call | flops 1000000000 | bytes 31850496 | tf_op jit(solution)/shard_map/finish/pallas_call | solution.py:475
  347.2 3.3 collective-permute-done
  350.5 2.4 fusion
Async XLA Ops:
  332.7 17.7 %collective-permute-start = (bf16[160,2304]{1,0:T(8,128)(2,1)}, bf16[160,2304]{1,0:T(8,128)(2,1)S(1)}, u32[]{:S(2)}, u32[]{:S(2)}) collective-permute-start(bf16[160,2304]{1,0:T(8,128)(2,1)} %get-tuple-element.20), channel_id=1, source_target_pairs={{2,0},{3,1},{4,6},{5,7},{10,8},{11,9},{12,14},{13,15},{18,16},{19,... | collective-permute-start | bytes 2211848 | tf_op jit(solution)/shard_map/ppermute | solution.py:520

commit v3 on v2

--- a/solution.py
+++ b/solution.py
@@ -366,11 +366,11 @@
                     mid_to_e(1, 2, h).start()
                 to_partner(1, 2, 3).start()
 
-            @pl.when((m == 3) & is_mid)
+            @pl.when((m == 2) & is_mid)
             def _():
                 send_v(1)
 
-            @pl.when(m == 3)
+            @pl.when((m == 3) & is_end)
             def _():
                 own_rows()
 
@@ -388,6 +388,7 @@
         @pl.when(is_mid)
         def _():
             send_w()
+            own_rows()
 
         flush([(accg, dwg_ref), (accu, dwu_ref)], stage)
 

time: 353 us -> 345 us (0.977)
  Pallas kernels: 345 us -> 336 us
    pallas_call x1, Pallas kernels: 332 us -> 323 us  [step(): pl.pallas_call(kernel, out_shape=outs, in_specs=[any_] * 7, out_specs=[an...]
where the time goes in v3:
time: 345 us; the launch traced here: 344 us
  Pallas kernels  336 us (97%)
  waiting for transfers between devices  4.36 us (1%)
    pallas_call x1, Pallas kernels, step(): pl.pallas_call(kernel, out_shape=outs, in_specs=[any_] * 7, out_specs=[an...  323 us
    pallas_call x1, Pallas kernels, finish(): pl.pallas_call(finish_kernel, in_specs=[any_] * 5, out_specs=[any_] * 4,...  13.1 us
  transfers between devices with their start and end apart: 1, of which 1 were waited for; matrix products, arithmetic and copies ran while one was open for 0% of the time, Pallas kernels for 4%

profile of v3, /device:TPU:0, one launch (start us, length us, event | category | flops | bytes accessed | tf_op | source)
XLA Modules:
  0.0 344.5 jit_solution(4661667433021180851)
XLA Ops:
  0.6 322.7 %mlp_backward.1 = (f32[480,2304]{1,0:T(8,128)}, bf16[2304,1152]{1,0:T(8,128)(2,1)}, bf16[2304,1152]{1,0:T(8,128)(2,1)}, bf16[1152,2304]{1,0:T(8,128)(2,1)}, bf16...) custom-call(bf16[480,2304]{1,0:T(8,128)(2,1)} %x_ref.1, ...), custom_call_target="tpu_custom_call" | custom-call | tf_op jit(solution)/shard_map/mlp_backward/pallas_call | solution.py:502
  323.3 1.3 collective-permute-start
  324.6 13.1 %finish.1 = (bf16[480,2304]{1,0:T(8,128)(2,1)}, bf16[2304,1152]{1,0:T(8,128)(2,1)}, bf16[2304,1152]{1,0:T(8,128)(2,1)}, bf16[1152,2304]{1,0:T(8,128)(2,1)}) custom-call(f32[480,2304]{1,0:T(8,128)} %get-tuple-element.14.base, bf16[320,2304]{1,0:T(8,128)(2,1)} %get-tuple-element.15.part, bf16[2304,1152]{1,0:T(8,128)(2,1)} %get-tuple-element.16.gate_in, ...), custom_call_target="tpu_custom_call" | custom-call | flops 1000000000 | bytes 31850496 | tf_op jit(solution)/shard_map/finish/pallas_call | solution.py:476
  337.8 4.4 %collective-permute-done = bf16[160,2304]{1,0:T(8,128)(2,1)S(1)} collective-permute-done((bf16[160,2304]{1,0:T(8,128)(2,1)}, bf16[160,2304]{1,0:T(8,128)(2,1)S(1)}, u32[]{:S(2)}, u32[]{:S(2)}) %collective-permute-start) | collective-permute-done | bytes 737312 | tf_op jit(solution)/shard_map/ppermute | solution.py:521
  342.1 2.4 fusion
Async XLA Ops:
  323.3 18.8 %collective-permute-start = (bf16[160,2304]{1,0:T(8,128)(2,1)}, bf16[160,2304]{1,0:T(8,128)(2,1)S(1)}, u32[]{:S(2)}, u32[]{:S(2)}) collective-permute-start(bf16[160,2304]{1,0:T(8,128)(2,1)} %get-tuple-element.20), channel_id=1, source_target_pairs={{2,0},{3,1},{4,6},{5,7},{10,8},{11,9},{12,14},{13,15},{18,16},{19,... | collective-permute-start | bytes 2211848 | tf_op jit(solution)/shard_map/ppermute | solution.py:521

commit v4 on v3

--- a/solution.py
+++ b/solution.py
@@ -12,6 +12,10 @@
 H = 3
 
 
+def last_rows(S):
+    return 16 * round(S / 60)
+
+
 def act(gate, up):
     return jax.nn.gelu(gate) * up
 
@@ -28,13 +32,15 @@
 
 
 def kernel(x_ref, dy_ref, gate_ref, up_ref, wg_ref, wu_ref, wd_ref,
-           base_ref, dwg_ref, dwu_ref, dwd_ref, rw, wlast,
+           base_ref, base_last, dwg_ref, dwu_ref, dwd_ref, rw, wlast,
            dyg, xg, dgs, dus, pown, pin, tst, ru, rv, rso,
            xv, gv, uv, pc, tc, rc, sc, oc, fc,
            sF, sE, rF, rE, sP, rP, sT, rT, sU, rU, sV, rV, sW, rW, lsem):
     S, D = x_ref.shape
     F = gate_ref.shape[1]
     C = S // H
+    L = last_rows(S)
+    B = (S - L) // 2
     tp = lax.axis_index("tp")
     z, c = tp // 2, tp % 2
     way = jnp.where(z < 2, 1, -1)
@@ -49,6 +55,7 @@
 
     partner = {"tp": 2 * z + 1 - c}
     rows = lambda h: pl.ds(h * C, C)
+    wrows = lambda i: pl.ds(i * B, B)
     given, gathered = (dy_ref, x_ref), (dyg, xg)
 
     def rcopy(src, dst, ssem, rsem, to):
@@ -97,20 +104,22 @@
     def v_copy(j, h):
         return rcopy(rso.at[j, rows(h)], rv.at[j, rows(h)], sV.at[j, h], rV.at[j, h], dev(1))
 
-    def w_copy(h):
-        return rcopy(rso.at[2, rows(h)], rw.at[rows(h)], sW.at[h], rW.at[h], dev(-1))
-
-    def combine(m, h, received, out, res=oc):
-        bufs = [pc, tc, rc, sc]
-        srcs = [pown.at[m, rows(h)], pin.at[m, rows(h)], *received]
+    def w_copy(i):
+        return rcopy(rso.at[2, wrows(i)], rw.at[wrows(i)], sW.at[i], rW.at[i], dev(-1))
+
+    def combine(m, at, received, out, res=oc):
+        n = at.size
+        bufs = [b.at[pl.ds(0, n)] for b in (pc, tc, rc, sc)]
+        res = res.at[pl.ds(0, n)]
+        srcs = [pown.at[m, at], pin.at[m, at], *received]
         local(*zip(srcs, bufs))
         step = 16
 
-        @pl.loop(0, C // step)
+        @pl.loop(0, n // step)
         def _(i):
             r = pl.ds(pl.multiple_of(i * step, step), step)
-            total = pc[r, :] + tc[r, :].astype(F32)
-            for b in bufs[2:len(srcs)]:
+            total = bufs[0][r, :]
+            for b in bufs[1:len(srcs)]:
                 total += b[r, :].astype(F32)
             res[r, :] = total.astype(res.dtype)
 
@@ -225,7 +234,7 @@
         def send_u(j):
             wait_term(j + 1)
             for h in range(H):
-                combine(j + 1, h, [], rso.at[j, rows(h)])
+                combine(j + 1, rows(h), [], rso.at[j, rows(h)])
                 u_copy(j, h).start()
 
         @pl.loop(0, 4)
@@ -307,35 +316,43 @@
 
     def own_rows():
         term(0).wait_recv()
+        parts = [(wrows(0), base_ref.at[wrows(0)]), (wrows(1), base_ref.at[wrows(1)]), (pl.ds(S - L, L), base_last)]
 
         @pl.when(is_mid)
         def _():
             for h in range(H):
                 rcopy(ru.at[0, rows(h)], ru.at[0, rows(h)], sU.at[0, h], rU.at[0, h], partner).wait_recv()
                 rcopy(rv.at[0, rows(h)], rv.at[0, rows(h)], sV.at[0, h], rV.at[0, h], partner).wait_recv()
-                combine(0, h, [ru.at[0, rows(h)], rv.at[0, rows(h)]], base_ref.at[rows(h)], fc)
+            for at, out in parts:
+                combine(0, at, [ru.at[0, at], rv.at[0, at]], out, fc)
 
         @pl.when(is_end)
         def _():
-            for h in range(H):
-                combine(0, h, [], base_ref.at[rows(h)], fc)
+            for at, out in parts:
+                combine(0, at, [], out, fc)
 
     def send_v(j):
         m = MID_M[j + 1]
         term(m).wait_recv()
         for h in range(H):
             rcopy(ru.at[j + 1, rows(h)], ru.at[j + 1, rows(h)], sU.at[j + 1, h], rU.at[j + 1, h], partner).wait_recv()
-            combine(m, h, [ru.at[j + 1, rows(h)]], rso.at[j, rows(h)])
+            combine(m, rows(h), [ru.at[j + 1, rows(h)]], rso.at[j, rows(h)])
             v_copy(j, h).start()
 
     def send_w():
         m = MID_M[-1]
         term(m).wait_recv()
-        for h in range(H):
-            rcopy(rv.at[1, rows(h)], rv.at[1, rows(h)], sV.at[1, h], rV.at[1, h], partner).wait_recv()
-            combine(m, h, [rv.at[1, rows(h)]], rso.at[2, rows(h)] if h < H - 1 else wlast)
-            if h < H - 1:
-                w_copy(h).start()
+        came = lambda h: rcopy(
+            rv.at[1, rows(h)], rv.at[1, rows(h)], sV.at[1, h], rV.at[1, h], partner).wait_recv()
+        came(0)
+        came(1)
+        combine(m, wrows(0), [rv.at[1, wrows(0)]], rso.at[2, wrows(0)])
+        w_copy(0).start()
+        came(2)
+        combine(m, wrows(1), [rv.at[1, wrows(1)]], rso.at[2, wrows(1)])
+        w_copy(1).start()
+        at = pl.ds(S - L, L)
+        combine(m, at, [rv.at[1, at]], wlast)
 
     def phase2(accg, accu, stage):
         accg[...] = jnp.zeros_like(accg)
@@ -399,11 +416,6 @@
         pltpu.VMEM((S, D), F32), pltpu.VMEM((S, D), BF16), pltpu.VMEM((2, tile_of(F, 128), D), BF16))
     pl.run_scoped(
         phase2, pltpu.VMEM((D, F), F32), pltpu.VMEM((D, F), F32), pltpu.VMEM((2, tile_of(D, 256), F), BF16))
-
-    @pl.when(is_end)
-    def _():
-        for h in range(H - 1):
-            rcopy(rw.at[rows(h)], rw.at[rows(h)], sW.at[h], rW.at[h], partner).wait_recv()
 
     for m in range(4):
         term(m).wait_send()
@@ -418,6 +430,8 @@
         for j in range(3):
             for h in range(H):
                 u_copy(j, h).wait_send()
+        for i in range(2):
+            rcopy(rw.at[wrows(i)], rw.at[wrows(i)], sW.at[i], rW.at[i], partner).wait_recv()
 
     @pl.when(is_mid)
     def _():
@@ -432,13 +446,13 @@
         for h in range(H):
             for j in range(2):
                 v_copy(j, h).wait_send()
-        for h in range(H - 1):
-            w_copy(h).wait_send()
+        for i in range(2):
+            w_copy(i).wait_send()
 
 
 def finish_kernel(base, part, gate_in, up_in, down_in, dx, gate_out, up_out, down_out, gv, uv, dv, bv, pv, ov, isem, osem):
     n = part.shape[0]
-    bring = [pltpu.make_async_copy(base.at[pl.ds(0, n)], bv, isem.at[0]), pltpu.make_async_copy(part, pv, isem.at[1])]
+    bring = [pltpu.make_async_copy(base, bv, isem.at[0]), pltpu.make_async_copy(part, pv, isem.at[1])]
     put = []
     for src, v, dst in ((gate_in, gv, gate_out), (up_in, uv, up_out), (down_in, dv, down_out)):
         size = src.shape[0] // 3
@@ -468,10 +482,9 @@
         cp.wait()
 
 
-def finish(base, part, *grads):
-    S, D = base.shape
+def finish(S, base, part, *grads):
+    n, D = base.shape
     any_ = pl.BlockSpec(memory_space=pl.ANY)
-    n = part.shape[0]
     moved = 2 * sum(g.size * 2 for g in grads)
     return pl.pallas_call(
         finish_kernel, in_specs=[any_] * 5, out_specs=[any_] * 4,
@@ -487,12 +500,14 @@
 def solution(mesh):
     def step(x, dy, gate, up, w_gate, w_up, w_down):
         (S, D), F = x.shape, gate.shape[1]
-        C = S // H
+        L = last_rows(S)
+        B = (S - L) // 2
         shape = jax.ShapeDtypeStruct
         any_ = pl.BlockSpec(memory_space=pl.ANY)
         outs = [
-            shape((S, D), F32), shape((D, F), BF16), shape((D, F), BF16), shape((F, D), BF16),
-            shape((S - C, D), BF16), shape((C, D), BF16),
+            shape((S - L, D), F32), shape((L, D), F32),
+            shape((D, F), BF16), shape((D, F), BF16), shape((F, D), BF16),
+            shape((S - L, D), BF16), shape((L, D), BF16),
             shape((8, S, D), BF16), shape((8, S, D), BF16),
             shape((8, S, F), BF16), shape((8, S, F), BF16),
             shape((4, S, D), F32), shape((4, S, D), BF16), shape((4, S, D), BF16),
@@ -506,23 +521,22 @@
             out_specs=[any_] * len(outs),
             scratch_shapes=[
                 pltpu.VMEM((S, D), BF16), pltpu.VMEM((S, F), BF16), pltpu.VMEM((S, F), BF16),
-                pltpu.VMEM((C, D), F32), pltpu.VMEM((C, D), BF16), pltpu.VMEM((C, D), BF16),
-                pltpu.VMEM((C, D), BF16), pltpu.VMEM((C, D), BF16), pltpu.VMEM((C, D), F32),
+                pltpu.VMEM((B, D), F32), pltpu.VMEM((B, D), BF16), pltpu.VMEM((B, D), BF16),
+                pltpu.VMEM((B, D), BF16), pltpu.VMEM((B, D), BF16), pltpu.VMEM((B, D), F32),
                 dma((2, 2, H)), dma((2, 3, H)), dma((2, 3, H)), dma((2, H)),
                 dma((2, 4)), dma((2, 4)), dma((4,)), dma((4,)),
-                dma((3, H)), dma((3, H)), dma((2, H)), dma((2, H)), dma((H,)), dma((H,)),
+                dma((3, H)), dma((3, H)), dma((2, H)), dma((2, H)), dma((2,)), dma((2,)),
                 dma((4,)),
             ],
             compiler_params=pltpu.CompilerParams(
                 collective_id=0, has_side_effects=True, vmem_limit_bytes=60 * 2**20),
             name="mlp_backward",
         )(x, dy, gate, up, w_gate, w_up, w_down)
-        base, dwg, dwu, dwd, early, last = out[:6]
+        base, base_last, dwg, dwu, dwd, early, last = out[:7]
         last = lax.ppermute(last, "tp", [(2, 0), (3, 1), (4, 6), (5, 7)])
-        dx, *grads = finish(base, early, dwg, dwu, dwd)
-        done = S - C
-        dx = lax.dynamic_update_slice(dx, (base[done:] + last.astype(F32)).astype(BF16), (done, 0))
-        return dx, *grads
+        dx, *grads = finish(S, base, early, dwg, dwu, dwd)
+        last = (base_last + last.astype(F32)).astype(BF16)
+        return lax.dynamic_update_slice(dx, last, (S - L, 0)), *grads
 
     both = P(("dp", "tp"), None)
     cols = P("dp", "tp")

time: 345 us -> 343 us (level)
  waiting for transfers between devices: 4.36 us -> 0.66 us
    ppermute x1, waiting for transfers between devices: 4.36 us -> 0.66 us  [step(): last = lax.ppermute(last, 'tp', [(2, 0), (3, 1), (4, 6), (5, 7)])]
where the time goes in v4:
time: 343 us
  Pallas kernels  339 us (99%)
    pallas_call x1, Pallas kernels, step(): pl.pallas_call(kernel, out_shape=outs, in_specs=[any_] * 7, out_specs=[an...  326 us
    pallas_call x1, Pallas kernels, finish(): pl.pallas_call(finish_kernel, in_specs=[any_] * 5, out_specs=[any_] * 4,...  13.5 us
  transfers between devices with their start and end apart: 1, of which 1 were waited for; matrix products, arithmetic and copies ran while one was open for 0% of the time, Pallas kernels for 4%

profile of v4, /device:TPU:0, one launch (start us, length us, event | category | flops | bytes accessed | tf_op | source)
XLA Modules:
  0.0 342.7 jit_solution(17858913455113757370)
XLA Ops:
  0.6 325.7 %mlp_backward.1 = (f32[352,2304]{1,0:T(8,128)}, f32[128,2304]{1,0:T(8,128)}, bf16[2304,1152]{1,0:T(8,128)(2,1)}, bf16[2304,1152]{1,0:T(8,128)(2,1)}, bf16[1152,2...) custom-call(bf16[480,2304]{1,0:T(8,128)(2,1)} %x_ref.1, ...), custom_call_target="tpu_custom_call" | custom-call | tf_op jit(solution)/shard_map/mlp_backward/pallas_call | solution.py:517
  326.4 1.3 collective-permute-start
  327.7 0.0 copy-start
  327.7 13.5 %finish.1 = (bf16[480,2304]{1,0:T(8,128)(2,1)}, bf16[2304,1152]{1,0:T(8,128)(2,1)}, bf16[2304,1152]{1,0:T(8,128)(2,1)}, bf16[1152,2304]{1,0:T(8,128)(2,1)}) custom-call(f32[352,2304]{1,0:T(8,128)} %get-tuple-element.15.base, bf16[352,2304]{1,0:T(8,128)(2,1)} %get-tuple-element.16.part, bf16[2304,1152]{1,0:T(8,128)(2,1)} %get-tuple-element.17.gate_in, ...), custom_call_target="tpu_custom_call" | custom-call | flops 1000000000 | bytes 31850496 | tf_op jit(solution)/shard_map/finish/pallas_call | solution.py:489
  341.2 0.7 collective-permute-done
  341.8 0.0 copy-done
  341.8 0.9 fusion
Async XLA Ops:
  326.4 15.4 %collective-permute-start = (bf16[128,2304]{1,0:T(8,128)(2,1)}, bf16[128,2304]{1,0:T(8,128)(2,1)S(1)}, u32[]{:S(2)}, u32[]{:S(2)}) collective-permute-start(bf16[128,2304]{1,0:T(8,128)(2,1)} %get-tuple-element.22), channel_id=1, source_target_pairs={{2,0},{3,1},{4,6},{5,7},{10,8},{11,9},{12,14},{13,15},{18,16},{19,... | collective-permute-start | bytes 1769480 | tf_op jit(solution)/shard_map/ppermute | solution.py:536
  327.7 14.1 %copy-start = (f32[128,2304]{1,0:T(8,128)S(1)}, f32[128,2304]{1,0:T(8,128)}, u32[]{:S(2)}) copy-start(f32[128,2304]{1,0:T(8,128)} %get-tuple-element.21) | copy-start | bytes 3538948

commit v5 on v4

--- a/solution.py
+++ b/solution.py
@@ -13,7 +13,7 @@
 
 
 def last_rows(S):
-    return 16 * round(S / 60)
+    return 16 * round(S / 48)
 
 
 def act(gate, up):
@@ -138,18 +138,21 @@
     def _():
         pl.semaphore_wait(barrier, 2)
 
-    @pl.when(is_mid)
-    def _():
-        for h in range(H):
-            mid_to_e(0, 0, h).start()
-            mid_to_f(0, 0, h).start()
-
-    @pl.when(is_end)
-    def _():
-        for h in range(H):
-            end_to_f(0, h).start()
-        for h in range(H):
-            end_to_f(1, h).start()
+    def first_sends(core):
+        @pl.when(is_mid & (c == core))
+        def _():
+            for h in range(H):
+                mid_to_e(0, 0, h).start()
+                mid_to_f(0, 0, h).start()
+
+        @pl.when(is_end & (c == core))
+        def _():
+            for h in range(H):
+                end_to_f(0, h).start()
+            for h in range(H):
+                end_to_f(1, h).start()
+
+    first_sends(1)
 
     for a in range(2):
         to_partner(a, 0, 0).start()
@@ -176,8 +179,9 @@
         return t
 
     def phase1(wd, wg, wu, accd, hid, dgv, duv, dxf, dxb, stage):
-        local((wd_ref, wd), (wg_ref, wg))
-        local((wu_ref, wu))
+        local((wd_ref, wd))
+        first_sends(0)
+        local((wg_ref, wg), (wu_ref, wu))
         accd[...] = jnp.zeros_like(accd)
 
         def unit(m, p):

time: 343 us -> 345 us (level)
  waiting for transfers between devices: 0.66 us -> 4.28 us
    ppermute x1, waiting for transfers between devices: 0.66 us -> 4.28 us  [step(): last = lax.ppermute(last, 'tp', [(2, 0), (3, 1), (4, 6), (5, 7)])]
where the time goes in v5:
time: 345 us; the launch traced here: 344 us
  Pallas kernels  336 us (97%)
  waiting for transfers between devices  4.28 us (1%)
    pallas_call x1, Pallas kernels, step(): pl.pallas_call(kernel, out_shape=outs, in_specs=[any_] * 7, out_specs=[an...  323 us
    pallas_call x1, Pallas kernels, finish(): pl.pallas_call(finish_kernel, in_specs=[any_] * 5, out_specs=[any_] * 4,...  13.2 us
  transfers between devices with their start and end apart: 1, of which 1 were waited for; matrix products, arithmetic and copies ran while one was open for 0% of the time, Pallas kernels for 4%

profile of v5, /device:TPU:0, one launch (start us, length us, event | category | flops | bytes accessed | tf_op | source)
XLA Modules:
  0.0 344.2 jit_solution(248329135532675505)
XLA Ops:
  0.6 322.6 %mlp_backward.1 = (f32[320,2304]{1,0:T(8,128)}, f32[160,2304]{1,0:T(8,128)}, bf16[2304,1152]{1,0:T(8,128)(2,1)}, bf16[2304,1152]{1,0:T(8,128)(2,1)}, bf16[1152,2...) custom-call(bf16[480,2304]{1,0:T(8,128)(2,1)} %x_ref.1, ...), custom_call_target="tpu_custom_call" | custom-call | tf_op jit(solution)/shard_map/mlp_backward/pallas_call | solution.py:521
  323.2 1.3 collective-permute-start
  324.5 0.0 copy-start
  324.5 13.2 %finish.1 = (bf16[480,2304]{1,0:T(8,128)(2,1)}, bf16[2304,1152]{1,0:T(8,128)(2,1)}, bf16[2304,1152]{1,0:T(8,128)(2,1)}, bf16[1152,2304]{1,0:T(8,128)(2,1)}) custom-call(f32[320,2304]{1,0:T(8,128)} %get-tuple-element.15.base, bf16[320,2304]{1,0:T(8,128)(2,1)} %get-tuple-element.16.part, bf16[2304,1152]{1,0:T(8,128)(2,1)} %get-tuple-element.17.gate_in, ...), custom_call_target="tpu_custom_call" | custom-call | flops 1000000000 | bytes 31850496 | tf_op jit(solution)/shard_map/finish/pallas_call | solution.py:493
  337.8 4.3 %collective-permute-done = bf16[160,2304]{1,0:T(8,128)(2,1)} collective-permute-done((bf16[160,2304]{1,0:T(8,128)(2,1)}, bf16[160,2304]{1,0:T(8,128)(2,1)}, u32[]{:S(2)}, u32[]{:S(2)}) %collective-permute-start) | collective-permute-done | bytes 737312 | tf_op jit(solution)/shard_map/ppermute | solution.py:540
  342.1 0.0 copy-done
  342.1 2.1 fusion
Async XLA Ops:
  323.2 18.8 %collective-permute-start = (bf16[160,2304]{1,0:T(8,128)(2,1)}, bf16[160,2304]{1,0:T(8,128)(2,1)}, u32[]{:S(2)}, u32[]{:S(2)}) collective-permute-start(bf16[160,2304]{1,0:T(8,128)(2,1)} %get-tuple-element.22), channel_id=1, source_target_pairs={{2,0},{3,1},{4,6},{5,7},{10,8},{11,9},{12,14},{13,15},{18,16},{19,... | collective-permute-start | bytes 2211848 | tf_op jit(solution)/shard_map/ppermute | solution.py:540
  324.5 17.6 %copy-start = (f32[160,2304]{1,0:T(8,128)S(1)}, f32[160,2304]{1,0:T(8,128)}, u32[]{:S(2)}) copy-start(f32[160,2304]{1,0:T(8,128)} %get-tuple-element.21) | copy-start | bytes 4423684
